TPU v7x, 16 devices: a whole 2x2x2 slice. The times are simulated.
16 devices in a mesh: tp: 2 (over z), dp: 8 (over y, x, core).
Axes of the slice: x: 2, y: 2, z: 2, core: 2. Of those that a mesh axis runs over, the one named last changes fastest.
Arguments:
- x_in: bfloat16 [4096, 2048], P('dp')
- w_gate: bfloat16 [2048, 5632], P('dp', 'tp')
- w_up: bfloat16 [2048, 5632], P('dp', 'tp')
- w_down: bfloat16 [5632, 2048], P('tp', 'dp')
- dy_in: bfloat16 [4096, 2048], P('dp')
Outputs:
- output 1: bfloat16 [4096, 2048], P('dp')
- output 2: bfloat16 [4096, 2048], P('dp')
- output 3: float32 [2048, 5632], P('dp', 'tp')
- output 4: float32 [2048, 5632], P('dp', 'tp')
- output 5: float32 [5632, 2048], P('tp', 'dp')
All inputs are finite; a program needn't handle non-finite values.
Results may differ from a plain program's by a relative error of at most 0.001.
Values are sent between devices in bfloat16 or wider.
A program may use at most 1 GiB of HBM per device.

v0:
```python
import jax
import jax.numpy as jnp
from jax import lax
from jax.sharding import PartitionSpec as P


def solution(mesh):
    def device_pass(x_rows, gate_blk, up_blk, down_blk, dy_rows):
        x_cols = lax.all_to_all(x_rows, 'dp', 1, 0, tiled=True)
        gate_part = jnp.dot(x_cols, gate_blk, preferred_element_type=jnp.float32)
        up_part = jnp.dot(x_cols, up_blk, preferred_element_type=jnp.float32)
        gate_pre = lax.psum_scatter(gate_part, 'dp', scatter_dimension=0, tiled=True)
        up_pre = lax.psum_scatter(up_part, 'dp', scatter_dimension=0, tiled=True)
        sig_gate = jax.nn.sigmoid(gate_pre)
        silu_gate = gate_pre * sig_gate
        hidden = (silu_gate * up_pre).astype(jnp.bfloat16)
        hidden_all = lax.all_gather(hidden, 'dp', axis=0, tiled=True)
        out_part = jnp.dot(hidden_all, down_blk, preferred_element_type=jnp.float32)
        y_cols = (x_cols.astype(jnp.float32) + lax.psum(out_part, 'tp')).astype(jnp.bfloat16)
        y_rows = lax.all_to_all(y_cols, 'dp', 0, 1, tiled=True)
        dy_cols = lax.all_to_all(dy_rows, 'dp', 1, 0, tiled=True)
        grad_part = jnp.einsum('td,fd->tf', dy_cols, down_blk, preferred_element_type=jnp.float32)
        grad_h = lax.psum_scatter(grad_part, 'dp', scatter_dimension=0, tiled=True)
        d_gate = (grad_h * up_pre * sig_gate * (1.0 + gate_pre * (1.0 - sig_gate))).astype(jnp.bfloat16)
        d_up = (grad_h * silu_gate).astype(jnp.bfloat16)
        gate_all = lax.all_gather(d_gate, 'dp', axis=0, tiled=True)
        up_all = lax.all_gather(d_up, 'dp', axis=0, tiled=True)
        dx_part = (jnp.einsum('tf,df->td', gate_all, gate_blk, preferred_element_type=jnp.float32)
                   + jnp.einsum('tf,df->td', up_all, up_blk, preferred_element_type=jnp.float32))
        dx_cols = (dy_cols.astype(jnp.float32) + lax.psum(dx_part, 'tp')).astype(jnp.bfloat16)
        dx_rows = lax.all_to_all(dx_cols, 'dp', 0, 1, tiled=True)
        dw_gate = jnp.einsum('td,tf->df', x_cols, gate_all, preferred_element_type=jnp.float32)
        dw_up = jnp.einsum('td,tf->df', x_cols, up_all, preferred_element_type=jnp.float32)
        dw_down = jnp.einsum('tf,td->fd', hidden_all, dy_cols, preferred_element_type=jnp.float32)
        return y_rows, dx_rows, dw_gate, dw_up, dw_down

    row_spec = P('dp', None)
    weight_spec = P('dp', 'tp')
    down_spec = P('tp', 'dp')
    return jax.shard_map(device_pass, mesh=mesh,
                         in_specs=(row_spec, weight_spec, weight_spec, down_spec, row_spec),
                         out_specs=(row_spec, row_spec, weight_spec, weight_spec, down_spec),
                         check_vma=False)
```

profile of v0, /device:TPU:0, one launch (start us, length us, event | category | flops | bytes accessed | tf_op | source)
XLA Modules:
  0.0 1483.7 jit_solution(5582256682716856348)
XLA Ops:
  7.2 1.8 copy.22
  9.1 31.8 %all_to_all.76 = bf16[512,8,256]{2,0,1:T(8,128)(2,1)S(1)} all-to-all(bf16[512,8,256]{2,0,1:T(8,128)(2,1)S(1)} %bitcast.52), channel_id=1, replica_groups=mesh['tp'=2,'dp'=8] {'dp'}, dimensions={1} | all-to-all | bytes 4194304 | tf_op jit(solution)/shard_map/all_to_all | solution.py:21
  40.9 17.7 %fusion.4 = f32[4096,2816]{1,0:T(8,128)} fusion(bf16[4096,256]{1,0:T(8,128)(2,1)S(1)} %bitcast.50, bf16[2816,256]{1,0:T(8,128)(2,1)S(1)} %copy-done), kind=kOutput, calls=%fused_computation.15 | convolution fusion | flops 5905580032 | bytes 49676288 | tf_op jit(solution)/shard_map/td,fd->tf/dot_general | solution.py:22
  58.7 1.5 copy-done.5
  60.4 29.1 %all_to_all.77 = bf16[512,8,256]{2,0,1:T(8,128)(2,1)S(1)} all-to-all(bf16[512,8,256]{2,0,1:T(8,128)(2,1)S(1)} %bitcast.53), channel_id=1, replica_groups=mesh['tp'=2,'dp'=8] {'dp'}, dimensions={1} | all-to-all | bytes 4194304 | tf_op jit(solution)/shard_map/all_to_all | solution.py:9
  89.5 17.7 %fusion.2 = f32[4096,2816]{1,0:T(8,128)} fusion(bf16[4096,256]{1,0:T(8,128)(2,1)S(1)} %bitcast.46, bf16[256,2816]{1,0:T(8,128)(2,1)S(1)} %copy-done.6), kind=kOutput, calls=%fused_computation.13 | convolution fusion | flops 5905580032 | bytes 49676288 | tf_op jit(solution)/shard_map/dot_general | solution.py:11
  107.3 19.1 %fusion.1 = f32[4096,2816]{1,0:T(8,128)} fusion(bf16[4096,256]{1,0:T(8,128)(2,1)S(1)} %bitcast.47, bf16[256,2816]{1,0:T(8,128)(2,1)} %param.6), kind=kOutput, calls=%fused_computation.12 | convolution fusion | flops 5905580032 | bytes 49676288 | tf_op jit(solution)/shard_map/dot_general | solution.py:10
  126.5 189.4 %reduce-scatter.8.cloned.1.call-done = f32[512,2816]{1,0:T(8,128)} async-done(((f32[4096,2816]{1,0:T(8,128)}), f32[512,2816]{1,0:T(8,128)}) %reduce-scatter.8.cloned.1.call-update) | async-done | bytes 5767184 | tf_op jit(solution)/shard_map/reduce_scatter | solution.py:23
  315.9 261.5 %reduce-scatter.6.cloned.1.call-done = f32[512,2816]{1,0:T(8,128)} async-done(((f32[4096,2816]{1,0:T(8,128)}), f32[512,2816]{1,0:T(8,128)}) %reduce-scatter.6.cloned.1.call-update) | async-done | bytes 5767184 | tf_op jit(solution)/shard_map/reduce_scatter | solution.py:13
  577.3 261.5 %reduce-scatter.4.cloned.1.call-done = f32[512,2816]{1,0:T(8,128)} async-done(((f32[4096,2816]{1,0:T(8,128)}), f32[512,2816]{1,0:T(8,128)}) %reduce-scatter.4.cloned.1.call-update) | async-done | bytes 5767184 | tf_op jit(solution)/shard_map/reduce_scatter | solution.py:12
  838.8 10.1 multiply_convert_fusion
  849.0 0.5 all-gather.6.cloned.1.call-update
  849.6 0.5 all-gather.8.cloned.1.call-update
  850.3 111.3 %all-gather.4.cloned.1.call-done = bf16[4096,2816]{1,0:T(8,128)(2,1)} async-done(((bf16[512,2816]{1,0:T(8,128)(2,1)}), bf16[4096,2816]{1,0:T(8,128)(2,1)}) %all-gather.4.cloned.1.call-update) | async-done | bytes 23068688 | tf_op jit(solution)/shard_map/all_gather | solution.py:17
  961.7 13.3 fusion.3
  974.9 101.6 %all-gather.6.cloned.1.call-done = bf16[4096,2816]{1,0:T(8,128)(2,1)} async-done(((bf16[512,2816]{1,0:T(8,128)(2,1)}), bf16[4096,2816]{1,0:T(8,128)(2,1)}) %all-gather.6.cloned.1.call-update) | async-done | bytes 23068688 | tf_op jit(solution)/shard_map/all_gather | solution.py:26
  1076.5 12.6 fusion.5
  1089.1 102.3 %all-gather.8.cloned.1.call-done = bf16[4096,2816]{1,0:T(8,128)(2,1)} async-done(((bf16[512,2816]{1,0:T(8,128)(2,1)}), bf16[4096,2816]{1,0:T(8,128)(2,1)}) %all-gather.8.cloned.1.call-update) | async-done | bytes 23068688 | tf_op jit(solution)/shard_map/all_gather | solution.py:27
  1191.4 13.3 convolution_add_fusion
  1204.7 194.2 %all-reduce.3.cloned.1.call-done = (f32[4096,256]{1,0:T(8,128)}, f32[4096,256]{1,0:T(8,128)}) async-done(((f32[4096,256]{1,0:T(8,128)}, f32[4096,256]{1,0:T(8,128)}), (f32[4096,256]{1,0:T(8,128)}, f32[4096,256]{1,0:T(8,128)})) %all-reduce.3.cloned.1.call-update) | async-done | bytes 8388624 | tf_op jit(solution)/shard_map/psum | solution.py:19
  1398.9 4.7 add_convert_fusion
  1403.6 4.6 all-to-all-start.3
  1408.2 12.5 convolution_bitcast_fusion.1
  1420.7 1.9 add_convert_fusion.1
  1422.6 11.8 all-to-all-done.3
  1434.4 4.4 all-to-all-start.1
  1438.8 12.4 convolution_bitcast_fusion
  1451.2 3.4 copy.15
  1454.5 3.5 copy.14
  1458.1 12.3 fusion.6
  1470.4 3.3 copy.19
  1473.7 3.2 copy.18
  (29 shorter events, 0.7 us)
Async XLA Ops:
  7.2 33.7 %copy-start = (bf16[2816,256]{1,0:T(8,128)(2,1)S(1)}, bf16[2816,256]{1,0:T(8,128)(2,1)}, u32[]{:S(2)}) copy-start(bf16[2816,256]{1,0:T(8,128)(2,1)} %param.8) | copy-start | bytes 4325380
  7.2 308.7 %reduce-scatter.8.cloned.1.call-start = ((), (), s32[]{:S(2)}) async-start(), calls=%async_computation.10 | async-start | bytes 51904512 | tf_op jit(solution)/shard_map/reduce_scatter | solution.py:23
  40.9 17.8 %copy-start.2 = (bf16[512,8,256]{2,0,1:T(8,128)(2,1)}, bf16[512,8,256]{2,0,1:T(8,128)(2,1)S(1)}, u32[]{:S(2)}) copy-start(bf16[512,8,256]{2,0,1:T(8,128)(2,1)S(1)} %all_to_all.76) | copy-start | bytes 6291460
  58.6 1.6 copy-start.5
  58.7 518.7 %reduce-scatter.6.cloned.1.call-start = ((), (), s32[]{:S(2)}) async-start(), calls=%async_computation.8 | async-start | bytes 51904512 | tf_op jit(solution)/shard_map/reduce_scatter | solution.py:13
  60.4 29.2 %copy-start.6 = (bf16[256,2816]{1,0:T(8,128)(2,1)S(1)}, bf16[256,2816]{1,0:T(8,128)(2,1)}, u32[]{:S(2)}) copy-start(bf16[256,2816]{1,0:T(8,128)(2,1)} %param.7) | copy-start | bytes 4325380
  107.3 731.5 %reduce-scatter.4.cloned.1.call-start = ((), (), s32[]{:S(2)}) async-start(), calls=%async_computation.7 | async-start | bytes 51904512 | tf_op jit(solution)/shard_map/reduce_scatter | solution.py:12
  126.5 835.2 %all-gather.4.cloned.1.call-start = ((), (), s32[]{:S(2)}) async-start(), calls=%async_computation.9 | async-start | bytes 25952256 | tf_op jit(solution)/shard_map/all_gather | solution.py:17
  849.0 227.6 %all-gather.6.cloned.1.call-start = ((), (), s32[]{:S(2)}) async-start(), calls=%async_computation.11 | async-start | bytes 25952256 | tf_op jit(solution)/shard_map/all_gather | solution.py:26
  849.5 341.8 %all-gather.8.cloned.1.call-start = ((), (), s32[]{:S(2)}) async-start(), calls=%async_computation.12 | async-start | bytes 25952256 | tf_op jit(solution)/shard_map/all_gather | solution.py:27
  850.1 548.8 %all-reduce.3.cloned.1.call-start = ((), (), s32[]{:S(2)}) async-start(), calls=%async_computation.13 | async-start | bytes 16777216 | tf_op jit(solution)/shard_map/psum | solution.py:19
  974.9 216.4 %copy-start.7 = (bf16[256,2816]{1,0:T(8,128)(2,1)S(1)}, bf16[256,2816]{1,0:T(8,128)(2,1)}, u32[]{:S(2)}) copy-start(bf16[256,2816]{1,0:T(8,128)(2,1)} %param.7) | copy-start | bytes 4325380
  1403.6 30.9 %all-to-all-start.3 = ((bf16[8,512,256]{2,1,0:T(8,128)(2,1)}), bf16[8,512,256]{2,1,0:T(8,128)(2,1)}, u32[]{:S(2)}, u32[]{:S(2)}) async-start(bf16[8,512,256]{2,1,0:T(8,128)(2,1)} %bitcast.55), calls=%async_computation.6 | async-start | bytes 4194304 | tf_op jit(solution)/shard_map/all_to_all | solution.py:31
  1408.1 12.5 copy-start.4
  1434.4 39.3 %all-to-all-start.1 = ((bf16[8,512,256]{2,1,0:T(8,128)(2,1)}), bf16[8,512,256]{2,1,0:T(8,128)(2,1)}, u32[]{:S(2)}, u32[]{:S(2)}) async-start(bf16[8,512,256]{2,1,0:T(8,128)(2,1)} %bitcast.54), calls=%async_computation.3 | async-start | bytes 4194304 | tf_op jit(solution)/shard_map/all_to_all | solution.py:20
  1454.5 3.5 copy-start.3
  1470.4 6.5 copy-start.1
Sparse Core Ops, SparseCore 0:
  58.8 257.0 reduce-scatter.7
  319.5 257.8 reduce-scatter.5
  580.9 257.8 reduce-scatter.3
  849.1 112.5 all-gather.3
  963.9 112.5 all-gather.5
  1078.8 112.5 all-gather.7
  1204.9 194.0 all-reduce.2
where the time goes:
time: 1480 us
  waiting for transfers between devices  1230 us (83%)
  matrix products  131 us (9%)
  blocking collectives  61 us (4%)
  local copies, waits for them, and re-layouts  16.9 us (1%)
  other arithmetic  16.7 us (1%)
    reduce_scatter x1, waiting for transfers between devices, device_pass(): lax.psum_scatter(gate_part, 'dp', scatter_dimension=0, tiled=True)  261 us
    reduce_scatter x1, waiting for transfers between devices, device_pass(): up_pre = lax.psum_scatter(up_part, 'dp', scatter_dimension=0, tiled=True)  261 us
    psum x1, waiting for transfers between devices, device_pass(): lax.psum(out_part, 'tp')  194 us
    reduce_scatter x1, waiting for transfers between devices, device_pass(): grad_h = lax.psum_scatter(grad_part, 'dp', scatter_dimension=0, tiled=True)  189 us
    all_gather x1, waiting for transfers between devices, device_pass(): hidden_all = lax.all_gather(hidden, 'dp', axis=0, tiled=True)  111 us
    all_gather x1, waiting for transfers between devices, device_pass(): up_all = lax.all_gather(d_up, 'dp', axis=0, tiled=True)  102 us
    all_gather x1, waiting for transfers between devices, device_pass(): gate_all = lax.all_gather(d_gate, 'dp', axis=0, tiled=True)  102 us
    all_to_all x1, blocking collectives, device_pass(): dy_cols = lax.all_to_all(dy_rows, 'dp', 1, 0, tiled=True)  31.8 us
  transfers between devices with their start and end apart: 9, of which 8 were waited for; matrix products, arithmetic and copies ran while one was open for 8% of the time, Pallas kernels for 0%

commit v1 on v0

v1 whole, which is shorter than its diff:
```python
import functools

import jax
import jax.numpy as jnp
from jax import lax
from jax.experimental import pallas as pl
from jax.experimental.pallas import tpu as pltpu
from jax.sharding import PartitionSpec as P

MESH = pl.DeviceIdType.MESH
BF16, F32 = jnp.bfloat16, jnp.float32
D, FH, FQ, ROWS, TOK = 2048, 2816, 1408, 256, 512
SUB = 256
NN = (((1,), (0,)), ((), ()))
NT = (((1,), (1,)), ((), ()))


def dot(a, b, dims):
    return lax.dot_general(a, b, dims, preferred_element_type=F32)


def kernel(x_in, wg_in, wu_in, wd_in, dy_in,
           y_out, dx_out, dwg_out, dwu_out, dwd_out, x_all, dy_all,
           wg, wu, wd, acc, xb, dyb, hb, dab, dbb, pb, rc, rz, fb, xt, dyt,
           wl, ws, wr, xl, xs, xf, xd, xr, pr, cs, cr, zs, zr, bs, br, fl, ds, dr, dl):
    tp, dp = lax.axis_index('tp'), lax.axis_index('dp')
    core, xc, yc = lax.rem(dp, 2), lax.rem(lax.div(dp, 2), 2), lax.div(dp, 4)
    col = lax.div(dp, 2)

    def idx(yy, xx, cc):
        return yy * 4 + xx * 2 + cc

    def dev(yy, xx, cc):
        return (tp, idx(yy, xx, cc))

    partner = dev(yc, xc, 1 - core)
    zdev = (1 - tp, dp)

    barrier = pltpu.get_barrier_semaphore()
    peers = [partner, zdev] + [dev(yc, 1 - xc, cc) for cc in (0, 1)] + [dev(1 - yc, xc, cc) for cc in (0, 1)]
    for peer in peers:
        pl.semaphore_signal(barrier, inc=1, device_id=peer, device_id_type=MESH)
    pl.semaphore_wait(barrier, len(peers))

    def remote(src, dst, ssem, rsem, device):
        return pltpu.make_async_remote_copy(src_ref=src, dst_ref=dst, send_sem=ssem, recv_sem=rsem,
                                            device_id=device, device_id_type=MESH)

    def w_src(m, cc):
        if m == 2:
            return wd_in.at[pl.ds(pl.multiple_of(cc * FQ, 128), FQ), :]
        return (wg_in, wu_in)[m].at[:, pl.ds(pl.multiple_of(cc * FQ, 128), FQ)]

    def w_at(m, r):
        if m == 2:
            return wd.at[r]
        return (wg, wu)[m].at[pl.ds(pl.multiple_of(r * ROWS, ROWS), ROWS), :]

    def w_local(m):
        return pltpu.make_async_copy(w_src(m, core), w_at(m, dp), wl.at[m])

    def w_direct(m):
        out = [remote(w_src(m, 1 - core), w_at(m, dp), ws.at[m, 0], wr.at[m, 0], partner)]
        for cc in (0, 1):
            out.append(remote(w_src(m, cc), w_at(m, dp), ws.at[m, 1 + cc], wr.at[m, 1 + core], dev(yc, 1 - xc, cc)))
            out.append(remote(w_src(m, cc), w_at(m, dp), ws.at[m, 3 + cc], wr.at[m, 3 + core], dev(1 - yc, xc, cc)))
        return out

    rx, ry = idx(yc, 1 - xc, 0), idx(1 - yc, xc, 1)

    def w_forward(m):
        return [remote(w_at(m, rx), w_at(m, rx), ws.at[m, 5], wr.at[m, 5], dev(1 - yc, xc, core)),
                remote(w_at(m, ry), w_at(m, ry), ws.at[m, 6], wr.at[m, 6], dev(yc, 1 - xc, core))]

    def w_wait(m, slot):
        remote(w_at(m, dp), w_at(m, dp), ws.at[m, slot], wr.at[m, slot], partner).wait_recv()

    arrays = ((x_in, x_all, xb), (dy_in, dy_all, dyb))

    def rows(j):
        return pl.ds(pl.multiple_of(j * SUB, SUB), SUB)

    def t_at(a, rel, s, j):
        return arrays[a][1].at[rel * 2 + s, rows(j)]

    def t_own(a, j, k):
        src = arrays[a][0].at[rows(j)]
        rel = (1, 2, 0)[k]
        sem = pr.at[0, j, a] if k == 2 else xr.at[rel, j, a]
        return remote(src, t_at(a, rel, core, j), xs.at[j, a, k], sem,
                      (dev(yc, 1 - xc, core), dev(1 - yc, xc, core), partner)[k])

    def t_share(a, rel, j):
        return remote(t_at(a, rel, core, j), t_at(a, rel, core, j), xd.at[rel, j, a], pr.at[rel, j, a], partner)

    fwd_dev = dev(yc + (1 - core) * (1 - 2 * yc), xc + core * (1 - 2 * xc), core)

    def t_forward(a, j):
        return remote(t_at(a, 1 + core, core, j), t_at(a, 3, core, j), xf.at[j, a], xr.at[3, j, a], fwd_dev)

    def t_wait_own(a, rel, j):
        remote(t_at(a, rel, core, j), t_at(a, rel, core, j), xd.at[rel, j, a], xr.at[rel, j, a], partner).wait_recv()

    def t_load(a, rel, s, j):
        half = 0 if s == 'own' else 1
        source = core if s == 'own' else 1 - core
        return pltpu.make_async_copy(t_at(a, rel, source, j), arrays[a][2].at[pl.ds(half * SUB, SUB)], xl.at[half, a])

    def t_load_own(a, j):
        return pltpu.make_async_copy(arrays[a][0].at[rows(j)], arrays[a][2].at[pl.ds(0, SUB)], xl.at[0, a])

    def gates(a, b, g):
        s = jax.nn.sigmoid(a)
        silu = a * s
        return ((silu * b).astype(BF16), (g * b * s * (1.0 + a * (1.0 - s))).astype(BF16), (g * silu).astype(BF16))

    def tiles(body):
        def step(n, carry):
            body(pl.ds(pl.multiple_of(n * 256, 256), 256))
            return carry
        lax.fori_loop(0, FQ // 256, step, 0)
        body(pl.ds(FQ // 256 * 256, FQ % 256))

    def grad_tile(r, cols):
        g = dot(dyb[r, 0:ROWS], wd[0, cols, :], NT)
        for i in range(1, 8):
            g = g + dot(dyb[r, i * ROWS:(i + 1) * ROWS], wd[i, cols, :], NT)
        return g

    def phase1(r):
        def body(cols):
            a = dot(xb[r, :], wg[:, cols], NN)
            b = dot(xb[r, :], wu[:, cols], NN)
            g = grad_tile(r, cols)
            hb[r, cols], dab[r, cols], dbb[r, cols] = gates(a, b, g)
        tiles(body)

    def weight_grads(r, size):
        own_cols = pl.ds(pl.multiple_of(col * 512, 512), 512)
        xt[:, 0:size] = xb[r, own_cols].T
        dyt[:, 0:size] = dyb[r, own_cols].T

        def body(cols):
            acc[0, :, cols] += dot(xt[:, 0:size], dab[r, cols], NN)
            acc[1, :, cols] += dot(xt[:, 0:size], dbb[r, cols], NN)
            acc[2, :, cols] += dot(dyt[:, 0:size], hb[r, cols], NN)
        tiles(body)

    def partial_out():
        def step(i, carry):
            cols = pl.ds(pl.multiple_of(i * ROWS, ROWS), ROWS)
            pb[0, :, cols] = dot(hb[...], wd[i], NN)
            pb[1, :, cols] = dot(dab[...], wg[cols, :], NT) + dot(dbb[...], wu[cols, :], NT)
            return carry
        lax.fori_loop(0, 8, step, 0)

    def c_send(p, a):
        return remote(pb.at[a, pl.ds(SUB, SUB)], rc.at[p, a], cs.at[p, a], cr.at[p, a], partner)

    def z_send(p, a):
        return remote(rc.at[p, a, pl.ds(pl.multiple_of((1 - tp) * 128, 128), 128)], rz.at[p, a],
                      zs.at[p, a], zr.at[p, a], zdev)

    outs = (y_out, dx_out)

    def out_rows(p, half):
        return pl.ds(pl.multiple_of(p * SUB + half * 128, 128), 128)

    def b_send(p, a):
        return remote(fb.at[p, a], outs[a].at[out_rows(p, tp)], bs.at[p, a], br.at[p, a], zdev)

    def b_local(p, a):
        return pltpu.make_async_copy(fb.at[p, a], outs[a].at[out_rows(p, tp)], fl.at[p, a])

    def c_reduce(p):
        src = (xb, dyb)
        for a in (0, 1):
            c_send(p, a).wait_recv()
            def step(i, carry):
                rr = pl.ds(pl.multiple_of(i * 32, 32), 32)
                rc[p, a, rr, :] = rc[p, a, rr, :] + pb[a, rr, :]
                return carry
            lax.fori_loop(0, SUB // 32, step, 0)
            z_send(p, a).start()
            keep = pl.multiple_of(tp * 128, 128)
            def step2(i, carry):
                rr = pl.ds(pl.multiple_of(keep + i * 32, 32), 32)
                rc[p, a, rr, :] = rc[p, a, rr, :] + src[a][rr, :].astype(F32)
                return carry
            lax.fori_loop(0, 4, step2, 0)

    def finalize(p, a):
        z_send(p, a).wait_recv()
        keep = pl.multiple_of(tp * 128, 128)
        def step(i, carry):
            rr = pl.ds(pl.multiple_of(i * 32, 32), 32)
            kr = pl.ds(pl.multiple_of(keep + i * 32, 32), 32)
            fb[p, a, rr, :] = (rc[p, a, kr, :] + rz[p, a, rr, :]).astype(BF16)
            return carry
        lax.fori_loop(0, 4, step, 0)
        b_send(p, a).start()
        b_local(p, a).start()

    for m in (0, 1, 2):
        w_local(m).start()
    for m in (0, 1):
        for c in w_direct(m):
            c.start()
    for j in (0, 1):
        for a in (0, 1):
            t_own(a, j, 2).start()
    for a in (0, 1):
        t_load_own(a, 0).start()

    def zero(i, carry):
        acc[:, pl.ds(pl.multiple_of(i * 32, 32), 32), :] = jnp.zeros((3, 32, FQ), F32)
        return carry
    lax.fori_loop(0, 16, zero, 0)

    for m in (0, 1):
        w_wait(m, 1)
        w_wait(m, 4)
        for c in w_forward(m):
            c.start()
    for c in w_direct(2):
        c.start()

    for a in (0, 1):
        t_own(a, 0, 2).wait_recv()
        t_load(a, 0, 'partner', 0).start()
    for m in (0, 1):
        w_local(m).wait()
        for slot in (0, 2, 3, 5, 6):
            w_wait(m, slot)
    for half in (0, 1):
        pltpu.make_async_copy(x_in.at[rows(0)], xb.at[pl.ds(half * SUB, SUB)], xl.at[half, 0]).wait()
        pltpu.make_async_copy(x_in.at[rows(0)], dyb.at[pl.ds(half * SUB, SUB)], xl.at[half, 1]).wait()

    everything = pl.ds(0, 2 * SUB)

    def early(cols):
        a = dot(xb[...], wg[:, cols], NN)
        b = dot(xb[...], wu[:, cols], NN)
        pb[0, :, cols], pb[1, :, cols] = a, b
    tiles(early)

    w_wait(2, 1)
    w_wait(2, 4)
    for c in w_forward(2):
        c.start()
    for j in (0, 1):
        for a in (0, 1):
            for k in (0, 1):
                t_own(a, j, k).start()
    w_local(2).wait()
    for slot in (0, 2, 3, 5, 6):
        w_wait(2, slot)

    def late(cols):
        g = grad_tile(everything, cols)
        hb[:, cols], dab[:, cols], dbb[:, cols] = gates(pb[0, :, cols], pb[1, :, cols], g)
    tiles(late)
    partial_out()
    for a in (0, 1):
        c_send(0, a).start()
    weight_grads(everything, 512)
    c_reduce(0)

    for a in (0, 1):
        t_load_own(a, 1).start()
        t_own(a, 1, 2).wait_recv()
        t_load(a, 0, 'partner', 1).start()
    for a in (0, 1):
        for half in (0, 1):
            pltpu.make_async_copy(x_in.at[rows(0)], arrays[a][2].at[pl.ds(half * SUB, SUB)], xl.at[half, a]).wait()
    phase1(everything)
    for a in (0, 1):
        c_send(0, a).wait_send()
    partial_out()
    for a in (0, 1):
        c_send(1, a).start()
    weight_grads(everything, 512)
    c_reduce(1)

    def block(k):
        first = (k + 2) // 2
        mid = (first * (3 - first)) // 2
        e = lax.rem(k, 2)
        return mid * (1 + e) + (1 - mid) * first, mid * (first - 1) + (1 - mid) * e

    def service(k):
        rel, j = block(k)
        for a in (0, 1):
            t_wait_own(a, rel, j)
            t_share(a, rel, j).start()
            t_load(a, rel, 'own', j).start()
        @pl.when(rel == 1 + core)
        def _():
            for a in (0, 1):
                t_forward(a, j).start()

    service(jnp.int32(0))

    def unit(t, carry):
        k, s = lax.div(t, 2), lax.rem(t, 2)

        @pl.when(s == 0)
        def _():
            rel, j = block(k)
            for a in (0, 1):
                t_share(a, rel, j).wait_recv()
                t_load(a, rel, 'partner', j).start()

        @pl.when(jnp.logical_and(s == 1, k < 5))
        def _():
            service(k + 1)

        for a in (0, 1):
            pltpu.make_async_copy(x_in.at[rows(0)], arrays[a][2].at[pl.ds(pl.multiple_of(s * SUB, SUB), SUB)],
                                  xl.at[s, a]).wait()
        r = pl.ds(pl.multiple_of(s * SUB, SUB), SUB)
        phase1(r)
        weight_grads(r, SUB)

        for q in range(4):
            @pl.when(t == 2 * q + 2)
            def _():
                finalize(q // 2, q % 2)
        return carry
    lax.fori_loop(0, 12, unit, 0)

    grads = (dwg_out, dwu_out, dwd_out)

    def g_part(n, c):
        return acc.at[n, pl.ds(pl.multiple_of(c * ROWS, ROWS), ROWS), :]

    def g_at(n):
        return grads[n].at[:, pl.ds(pl.multiple_of(core * FQ, 128), FQ)]

    g_send = [remote(g_part(n, 1 - core), g_at(n), ds.at[n], dr.at[n], partner) for n in range(3)]
    g_local = [pltpu.make_async_copy(g_part(n, core), g_at(n), dl.at[n]) for n in range(3)]
    for n in range(3):
        g_send[n].start()
        g_local[n].start()

    for m in (0, 1, 2):
        for c in w_direct(m) + w_forward(m):
            c.wait_send()
    for a in (0, 1):
        for j in (0, 1):
            for k in (0, 1, 2):
                t_own(a, j, k).wait_send()
            t_forward(a, j).wait_send()
            for rel in (1, 2, 3):
                t_share(a, rel, j).wait_send()
        c_send(1, a).wait_send()
        for p in (0, 1):
            z_send(p, a).wait_send()
            b_local(p, a).wait()
            b_send(p, a).wait()
    for n in range(3):
        g_local[n].wait()
        g_send[n].wait()


def solution(mesh):
    sds = jax.ShapeDtypeStruct
    dma, vmem = pltpu.SemaphoreType.DMA, pltpu.VMEM

    def device_pass(x, wg, wu, wd, dy):
        anyspec = pl.BlockSpec(memory_space=pl.ANY)
        out = pl.pallas_call(
            kernel,
            out_shape=[sds((TOK, D), BF16), sds((TOK, D), BF16), sds((ROWS, FH), F32), sds((ROWS, FH), F32),
                       sds((ROWS, FH), F32), sds((8, TOK, D), BF16), sds((8, TOK, D), BF16)],
            in_specs=[anyspec] * 5,
            out_specs=[anyspec] * 7,
            scratch_shapes=[
                vmem((D, FQ), BF16), vmem((D, FQ), BF16), vmem((8, FQ, ROWS), BF16),
                vmem((3, 512, FQ), F32),
                vmem((2 * SUB, D), BF16), vmem((2 * SUB, D), BF16),
                vmem((2 * SUB, FQ), BF16), vmem((2 * SUB, FQ), BF16), vmem((2 * SUB, FQ), BF16),
                vmem((2, 2 * SUB, D), F32), vmem((2, 2, SUB, D), F32), vmem((2, 2, 128, D), F32),
                vmem((2, 2, 128, D), BF16),
                vmem((512, 2 * SUB), BF16), vmem((512, 2 * SUB), BF16),
                dma((3,)), dma((3, 7)), dma((3, 7)),
                dma((2, 2)), dma((2, 2, 3)), dma((2, 2)), dma((4, 2, 2)), dma((4, 2, 2)), dma((4, 2, 2)),
                dma((2, 2)), dma((2, 2)), dma((2, 2)), dma((2, 2)), dma((2, 2)), dma((2, 2)), dma((2, 2)),
                dma((3,)), dma((3,)), dma((3,)),
            ],
            compiler_params=pltpu.CompilerParams(collective_id=0, has_side_effects=True,
                                                 vmem_limit_bytes=67043328),
        )(x, wg, wu, wd, dy)
        return out[0], out[1], out[2], out[3], out[4].T

    row_spec = P('dp', None)
    weight_spec = P('dp', 'tp')
    down_spec = P('tp', 'dp')
    return jax.shard_map(device_pass, mesh=mesh,
                         in_specs=(row_spec, weight_spec, weight_spec, down_spec, row_spec),
                         out_specs=(row_spec, row_spec, weight_spec, weight_spec, down_spec),
                         check_vma=False)
```

time: 1480 us -> 333 us (0.23)
  waiting for transfers between devices: 1230 us -> 0 us
  Pallas kernels: 0 us -> 319 us
  matrix products: 131 us -> 0 us
  blocking collectives: 61 us -> 0 us
  other arithmetic: 16.7 us -> 0 us
    reduce_scatter x3 -> x0, waiting for transfers between devices: 712 us -> none  [the longest x1 261 us: device_pass(): lax.psum_scatter(gate_part, 'dp', scatter_dimension=0, tiled=True)]
    pallas_call x0 -> x1, Pallas kernels: none -> 319 us  [device_pass(): pl.pallas_call(kernel, out_shape=[sds((TOK, D), BF16), sds((TOK, D), BF16...]
    all_gather x3 -> x0, waiting for transfers between devices: 315 us -> none  [the longest x1 111 us: device_pass(): hidden_all = lax.all_gather(hidden, 'dp', axis=0, tiled=True)]
    psum x1 -> x0, waiting for transfers between devices: 194 us -> none  [device_pass(): lax.psum(out_part, 'tp')]
    dot_general x9 -> x0, matrix products: 131 us -> none  [the longest x1 19.1 us: device_pass(): gate_part = jnp.dot(x_cols, gate_blk, preferred_element_type=jnp.float32)]
    all_to_all x2 -> x0, blocking collectives: 61 us -> none  [the longest x1 31.8 us: device_pass(): dy_cols = lax.all_to_all(dy_rows, 'dp', 1, 0, tiled=True)]
    convert_element_type x3 -> x0, other arithmetic: 16.7 us -> none  [the longest x1 10.1 us: device_pass(): d_up = (grad_h * silu_gate).astype(jnp.bfloat16)]
  transfers between devices with their start and end apart: 9 -> 0, of which waited for: 8 -> 0; matrix products, arithmetic and copies ran while one was open for 8% -> 0% of each run, Pallas kernels for 0% -> 0%
where the time goes in v1:
time: 333 us; the launch traced here: 332 us
  Pallas kernels  319 us (96%)
  local copies, waits for them, and re-layouts  12.9 us (4%)
    pallas_call x1, Pallas kernels, device_pass(): pl.pallas_call(kernel, out_shape=[sds((TOK, D), BF16), sds((TOK, D), BF16...  319 us
    unnamed x13, local copies, waits for them, and re-layouts  12.9 us

profile of v1, /device:TPU:0, one launch (start us, length us, event | category | flops | bytes accessed | tf_op | source)
XLA Modules:
  0.0 332.4 jit_solution(17599268589159018717)
XLA Ops:
  0.6 318.8 %shard_map.92 = (bf16[512,2048]{1,0:T(8,128)(2,1)}, bf16[512,2048]{1,0:T(8,128)(2,1)}, f32[256,2816]{1,0:T(8,128)}, f32[256,2816]{1,0:T(8,128)}, f32[256,2816]{1...) custom-call(bf16[512,2048]{1,0:T(8,128)(2,1)} %x_in.1, bf16[256,2816]{1,0:T(8,128)(2,1)} %wg_in.1, ...), custom_call_target="tpu_custom_call" | custom-call | tf_op jit(solution)/shard_map/pallas_call | solution.py:372
  319.5 0.0 copy-start.3
  319.5 3.5 %copy.10 = f32[2816,256]{1,0:T(8,128)} copy(f32[2816,256]{0,1:T(8,128)} %bitcast.1) | data formatting | bytes 5767168
  323.0 0.0 copy-done.3
  323.0 0.0 copy-start.2
  323.0 1.3 copy.15
  324.3 1.0 copy-done.2
  325.3 0.0 copy-start.1
  325.4 1.3 copy.16
  326.7 1.3 copy-done.1
  327.9 0.0 copy-start
  327.9 1.6 copy.17
  329.5 1.3 copy-done
  330.8 1.6 copy.18
Async XLA Ops:
  319.5 3.5 %copy-start.3 = (bf16[512,2048]{1,0:T(8,128)(2,1)S(1)}, bf16[512,2048]{1,0:T(8,128)(2,1)}, u32[]{:S(2)}) copy-start(bf16[512,2048]{1,0:T(8,128)(2,1)} %get-tuple-element.25) | copy-start | bytes 6291460
  323.0 2.3 copy-start.2
  325.3 2.6 copy-start.1
  327.9 2.9 copy-start

commit v2 on v1

v2 whole, which is shorter than its diff:
```python
import functools

import jax
import jax.numpy as jnp
from jax import lax
from jax.experimental import pallas as pl
from jax.experimental.pallas import tpu as pltpu
from jax.sharding import PartitionSpec as P

MESH = pl.DeviceIdType.MESH
BF16, F32 = jnp.bfloat16, jnp.float32
D, FH, FQ, ROWS, TOK = 2048, 2816, 1408, 256, 512
SUB, BLK, PIECES = 128, 256, 4
NN = (((1,), (0,)), ((), ()))
NT = (((1,), (1,)), ((), ()))


def dot(a, b, dims):
    return lax.dot_general(a, b, dims, preferred_element_type=F32)


def kernel(x_in, wg_in, wu_in, wd_in, dy_in,
           y_out, dx_out, dwg_out, dwu_out, dwd_out, x_all, dy_all,
           wg, wu, wd, acc, xb, dyb, hb, dab, dbb, pb, rc, rz, fb, xt, dyt,
           wl, ws, wr, xl, os, orr, xs, xf, xd, xr, pr, ys, yr, vs, vr, cs, cr, zs, zr, bs, br, fl, ds, dr, dl):
    tp, dp = lax.axis_index('tp'), lax.axis_index('dp')
    core, xc, yc = lax.rem(dp, 2), lax.rem(lax.div(dp, 2), 2), lax.div(dp, 4)
    col = lax.div(dp, 2)

    def idx(yy, xx, cc):
        return yy * 4 + xx * 2 + cc

    def dev(yy, xx, cc):
        return (tp, idx(yy, xx, cc))

    partner = dev(yc, xc, 1 - core)
    zdev = (1 - tp, dp)

    barrier = pltpu.get_barrier_semaphore()
    peers = [partner, zdev] + [dev(yc, 1 - xc, cc) for cc in (0, 1)] + [dev(1 - yc, xc, cc) for cc in (0, 1)]
    for peer in peers:
        pl.semaphore_signal(barrier, inc=1, device_id=peer, device_id_type=MESH)
    pl.semaphore_wait(barrier, len(peers))

    def remote(src, dst, ssem, rsem, device):
        return pltpu.make_async_remote_copy(src_ref=src, dst_ref=dst, send_sem=ssem, recv_sem=rsem,
                                            device_id=device, device_id_type=MESH)

    def w_src(m, cc):
        if m == 2:
            return wd_in.at[pl.ds(pl.multiple_of(cc * FQ, 128), FQ), :]
        return (wg_in, wu_in)[m].at[:, pl.ds(pl.multiple_of(cc * FQ, 128), FQ)]

    def w_at(m, r):
        if m == 2:
            return wd.at[r]
        return (wg, wu)[m].at[pl.ds(pl.multiple_of(r * ROWS, ROWS), ROWS), :]

    def w_local(m):
        return pltpu.make_async_copy(w_src(m, core), w_at(m, dp), wl.at[m])

    def w_direct(m):
        out = [remote(w_src(m, 1 - core), w_at(m, dp), ws.at[m, 0], wr.at[m, 0], partner)]
        for cc in (0, 1):
            out.append(remote(w_src(m, cc), w_at(m, dp), ws.at[m, 1 + cc], wr.at[m, 1 + core], dev(yc, 1 - xc, cc)))
            out.append(remote(w_src(m, cc), w_at(m, dp), ws.at[m, 3 + cc], wr.at[m, 3 + core], dev(1 - yc, xc, cc)))
        return out

    rx, ry = idx(yc, 1 - xc, 0), idx(1 - yc, xc, 1)

    def w_forward(m):
        return [remote(w_at(m, rx), w_at(m, rx), ws.at[m, 5], wr.at[m, 5], dev(1 - yc, xc, core)),
                remote(w_at(m, ry), w_at(m, ry), ws.at[m, 6], wr.at[m, 6], dev(yc, 1 - xc, core))]

    def w_wait(m, slot):
        remote(w_at(m, dp), w_at(m, dp), ws.at[m, slot], wr.at[m, slot], partner).wait_recv()

    arrays = ((x_in, x_all), (dy_in, dy_all))

    def rows(j, size=SUB):
        return pl.ds(pl.multiple_of(j * size, size), size)

    def t_at(a, rel, s, j):
        return arrays[a][1].at[rel * 2 + s, rows(j)]

    def t_partner(a, p):
        return remote(arrays[a][0].at[rows(p, BLK)], arrays[a][1].at[core, rows(p, BLK)],
                      os.at[p, a], orr.at[p, a], partner)

    def t_own(a, j, k):
        return remote(arrays[a][0].at[rows(j)], t_at(a, 1 + k, core, j), xs.at[j, a, k], xr.at[1 + k, j, a],
                      (dev(yc, 1 - xc, core), dev(1 - yc, xc, core))[k])

    def t_share(a, rel, j):
        return remote(t_at(a, rel, core, j), t_at(a, rel, core, j), xd.at[rel, j, a], pr.at[rel, j, a], partner)

    fwd_dev = dev(yc + (1 - core) * (1 - 2 * yc), xc + core * (1 - 2 * xc), core)

    def t_forward(a, j):
        return remote(t_at(a, 1 + core, core, j), t_at(a, 3, core, j), xf.at[j, a], xr.at[3, j, a], fwd_dev)

    def t_wait_own(a, rel, j):
        remote(t_at(a, rel, core, j), t_at(a, rel, core, j), xd.at[rel, j, a], xr.at[rel, j, a], partner).wait_recv()

    def p_loads(a, p, ref, sem):
        return [pltpu.make_async_copy(arrays[a][0].at[rows(p, BLK)], ref.at[pl.ds(0, BLK)], xl.at[sem, 0]),
                pltpu.make_async_copy(arrays[a][1].at[1 - core, rows(p, BLK)], ref.at[pl.ds(BLK, BLK)], xl.at[sem, 1])]

    bufs = (xb, dyb)

    def u_load(a, rel, j, half, slot):
        source = core if half == 0 else 1 - core
        return pltpu.make_async_copy(t_at(a, rel, source, j),
                                     bufs[a].at[pl.ds(pl.multiple_of(slot * BLK + half * SUB, SUB), SUB)],
                                     xl.at[4 + slot * 2 + half, a])

    def gates(a, b, g):
        s = jax.nn.sigmoid(a)
        silu = a * s
        return ((silu * b).astype(BF16), (g * b * s * (1.0 + a * (1.0 - s))).astype(BF16), (g * silu).astype(BF16))

    main, rest = FQ // 256, pl.ds(FQ // 256 * 256, FQ % 256)

    def tiles(body):
        def step(n, carry):
            body(pl.ds(pl.multiple_of(n * 256, 256), 256))
            return carry
        lax.fori_loop(0, main, step, 0)

    def grad_tile(dy, r, cols):
        g = dot(dy[r, 0:ROWS], wd[0, cols, :], NT)
        for i in range(1, 8):
            g = g + dot(dy[r, i * ROWS:(i + 1) * ROWS], wd[i, cols, :], NT)
        return g

    def rest_pair(x, r):
        both = dot(x[r, :], jnp.concatenate([wg[:, rest], wu[:, rest]], axis=1), NN)
        return both[:, 0:FQ % 256], both[:, FQ % 256:]

    def phase1(x, dy, r, o):
        def body(cols):
            a = dot(x[r, :], wg[:, cols], NN)
            b = dot(x[r, :], wu[:, cols], NN)
            hb[o, cols], dab[o, cols], dbb[o, cols] = gates(a, b, grad_tile(dy, r, cols))
        tiles(body)
        a, b = rest_pair(x, r)
        hb[o, rest], dab[o, rest], dbb[o, rest] = gates(a, b, grad_tile(dy, r, rest))

    def transposes(x, dy, r, size):
        own_cols = pl.ds(pl.multiple_of(col * 512, 512), 512)
        xt[:, 0:size] = x[r, own_cols].T
        dyt[:, 0:size] = dy[r, own_cols].T

    def weight_grads(size, first=False):
        o = pl.ds(0, size)

        def put(n, cols, value):
            acc[n, :, cols] = value if first else acc[n, :, cols] + value

        def body(cols):
            put(0, cols, dot(xt[:, 0:size], dab[o, cols], NN))
            put(1, cols, dot(xt[:, 0:size], dbb[o, cols], NN))
            put(2, cols, dot(dyt[:, 0:size], hb[o, cols], NN))
        tiles(body)
        both = dot(xt[:, 0:size], jnp.concatenate([dab[o, rest], dbb[o, rest]], axis=1), NN)
        put(0, rest, both[:, 0:FQ % 256])
        put(1, rest, both[:, FQ % 256:])
        put(2, rest, dot(dyt[:, 0:size], hb[o, rest], NN))

    cols_of = [pl.ds(pl.multiple_of(q * 512, 512), 512)
               for q in (col, yc * 2 + 1 - xc, (1 - yc) * 2 + xc, (1 - yc) * 2 + 1 - xc)]
    first_of = [q * 2 for q in (col, yc * 2 + 1 - xc, (1 - yc) * 2 + xc, (1 - yc) * 2 + 1 - xc)]

    def y_buf(p, rel):
        k = p * 4 + rel
        return (acc, k // 2, k % 2 * 512) if k < 6 else (pb, k - 6, FQ)

    def y_send(p, rel):
        ref, n, off = y_buf(p, rel)
        return remote(ref.at[n, pl.ds(BLK, BLK), pl.ds(off, 512)], rc.at[p, 0, :, cols_of[rel]],
                      ys.at[p, rel], yr.at[p, rel], partner)

    def y_zsend(p, rel):
        return remote(rc.at[p, 0, rows(1 - tp, 128), cols_of[rel]], rz.at[p, 0, :, cols_of[rel]],
                      vs.at[p, rel], vr.at[p, rel], zdev)

    def y_group(p, rel):
        ref, n, off = y_buf(p, rel)
        h = (hb, dbb)[p]

        def step(i, carry):
            ref[n, :, pl.ds(pl.multiple_of(off + i * ROWS, 128), ROWS)] = dot(h[...], wd[first_of[rel] + i], NN)
            return carry
        lax.fori_loop(0, 2, step, 0)
        y_send(p, rel).start()

    def add_rows(total, count, base, body):
        def step(i, carry):
            body(pl.ds(pl.multiple_of(base + i * count, count), count), i)
            return carry
        lax.fori_loop(0, total // count, step, 0)

    def y_finish(p, rel):
        ref, n, off = y_buf(p, rel)
        cols = cols_of[rel]
        y_send(p, rel).wait_recv()

        def both(rr, i):
            rc[p, 0, rr, cols] = rc[p, 0, rr, cols] + ref[n, rr, pl.ds(off, 512)]
        add_rows(BLK, 64, 0, both)
        y_zsend(p, rel).start()
        x = (xb, fb)[p]

        def keep(rr, i):
            rc[p, 0, rr, cols] = rc[p, 0, rr, cols] + x[rr, cols].astype(F32)
        add_rows(128, 64, tp * 128, keep)

    def dx_block(p):
        def step(i, carry):
            cols = pl.ds(pl.multiple_of(i * ROWS, ROWS), ROWS)
            pb[p, :, cols] = dot(dab[...], wg[cols, :], NT) + dot(dbb[...], wu[cols, :], NT)
            return carry
        lax.fori_loop(0, 8, step, 0)
        c_send(p).start()

    def c_send(p):
        return remote(pb.at[p, pl.ds(BLK, BLK)], rc.at[p, 1], cs.at[p], cr.at[p], partner)

    def z_send(p):
        return remote(rc.at[p, 1, rows(1 - tp, 128)], rz.at[p, 1], zs.at[p], zr.at[p], zdev)

    def dx_finish(p, dy):
        c_send(p).wait_recv()

        def both(rr, i):
            rc[p, 1, rr, :] = rc[p, 1, rr, :] + pb[p, rr, :]
        add_rows(BLK, 32, 0, both)
        z_send(p).start()

        def keep(rr, i):
            rc[p, 1, rr, :] = rc[p, 1, rr, :] + dy[rr, :].astype(F32)
        add_rows(128, 32, tp * 128, keep)

    outs = (y_out, dx_out)

    def out_rows(p, half):
        return pl.ds(pl.multiple_of(p * BLK + half * 128, 128), 128)

    def fb_at(p, a):
        return fb.at[rows(p * 2 + a, 128)]

    def b_send(p, a):
        return remote(fb_at(p, a), outs[a].at[out_rows(p, tp)], bs.at[p, a], br.at[p, a], zdev)

    def b_local(p, a):
        return pltpu.make_async_copy(fb_at(p, a), outs[a].at[out_rows(p, tp)], fl.at[p, a])

    def finalize(p, a):
        if a == 0:
            for rel in range(4):
                y_zsend(p, rel).wait_recv()
        else:
            z_send(p).wait_recv()

        def body(rr, i):
            kr = pl.ds(pl.multiple_of(tp * 128 + i * 32, 32), 32)
            fr = pl.ds(pl.multiple_of((p * 2 + a) * 128 + i * 32, 32), 32)
            fb[fr, :] = (rc[p, a, kr, :] + rz[p, a, rr, :]).astype(BF16)
        add_rows(128, 32, 0, body)
        b_send(p, a).start()
        b_local(p, a).start()

    for m in (0, 1, 2):
        w_local(m).start()
    for m in (0, 1):
        for c in w_direct(m):
            c.start()
    for p in (0, 1):
        for a in (0, 1):
            t_partner(a, p).start()
    for m in (0, 1):
        w_wait(m, 1)
        w_wait(m, 4)
        for c in w_forward(m):
            c.start()
    for c in w_direct(2):
        c.start()

    for p in (0, 1):
        for a in (0, 1):
            t_partner(a, p).wait_recv()
    first_loads = p_loads(0, 0, xb, 0) + p_loads(1, 0, dyb, 1) + p_loads(0, 1, fb, 2)
    for c in first_loads:
        c.start()
    for c in first_loads:
        c.wait()
    everything = pl.ds(0, 2 * BLK)
    transposes(xb, dyb, everything, 2 * BLK)

    for m in (0, 1):
        w_local(m).wait()
        for slot in (0, 2, 3, 5, 6):
            w_wait(m, slot)

    def silu_up(a, b):
        return (a * jax.nn.sigmoid(a) * b).astype(BF16)

    def early0(cols):
        a = dot(xb[...], wg[:, cols], NN)
        b = dot(xb[...], wu[:, cols], NN)
        pb[0, :, cols], pb[1, :, cols] = a, b
        hb[:, cols] = silu_up(a, b)
    tiles(early0)
    a, b = rest_pair(xb, everything)
    pb[0, :, rest], pb[1, :, rest] = a, b
    hb[:, rest] = silu_up(a, b)
    w_local(2).wait()
    w_wait(2, 0)
    y_group(0, 0)

    def early1(cols):
        a = dot(fb[...], wg[:, cols], NN)
        b = dot(fb[...], wu[:, cols], NN)
        dbb[:, cols] = silu_up(a, b)
    tiles(early1)
    a, b = rest_pair(fb, everything)
    dbb[:, rest] = silu_up(a, b)
    y_finish(0, 0)
    y_group(1, 0)

    w_wait(2, 1)
    w_wait(2, 4)
    for c in w_forward(2):
        c.start()
    for j in range(PIECES):
        for a in (0, 1):
            for k in (0, 1):
                t_own(a, j, k).start()
    y_finish(1, 0)
    w_wait(2, 2)
    y_group(0, 1)
    y_group(1, 1)
    w_wait(2, 3)
    y_finish(0, 1)
    y_group(0, 2)
    y_finish(1, 1)
    y_group(1, 2)
    y_finish(0, 2)
    y_finish(1, 2)
    w_wait(2, 5)
    w_wait(2, 6)
    y_group(0, 3)
    y_group(1, 3)

    def late(cols):
        _, dab[:, cols], dbb[:, cols] = gates(pb[0, :, cols], pb[1, :, cols], grad_tile(dyb, everything, cols))
    y_finish(0, 3)
    tiles(late)
    late(rest)
    y_finish(1, 3)
    for p in (0, 1):
        for rel in range(4):
            y_send(p, rel).wait_send()
    dy1_loads = p_loads(1, 1, xb, 0)
    for c in dy1_loads:
        c.start()
    dx_block(0)
    weight_grads(2 * BLK, first=True)
    dx_finish(0, dyb)
    for c in dy1_loads:
        c.wait()
    transposes(fb, xb, everything, 2 * BLK)
    phase1(fb, xb, everything, everything)
    dx_block(1)
    finalize(0, 0)
    weight_grads(2 * BLK)
    dx_finish(1, xb)
    finalize(1, 0)

    def unit_of(k):
        late_unit = k // (2 * PIECES)
        return ((1 - late_unit) * (1 + lax.rem(k, 2)) + late_unit * 3,
                (1 - late_unit) * (k // 2) + late_unit * (k - 2 * PIECES))

    def service(k):
        rel, j = unit_of(k)
        slot = lax.rem(k, 2)
        for a in (0, 1):
            t_wait_own(a, rel, j)
            t_share(a, rel, j).start()
            u_load(a, rel, j, 0, slot).start()

        @pl.when(rel == 1 + core)
        def _():
            for a in (0, 1):
                t_forward(a, j).start()

    def other_half(k):
        rel, j = unit_of(k)
        slot = lax.rem(k, 2)
        for a in (0, 1):
            t_share(a, rel, j).wait_recv()
            u_load(a, rel, j, 1, slot).start()

    service(jnp.int32(0))
    other_half(jnp.int32(0))

    def unit(k, carry):
        rel, j = unit_of(k)
        slot = lax.rem(k, 2)
        ahead = k < 2 * PIECES

        @pl.when(ahead)
        def _():
            service(k + 1)

        for half in (0, 1):
            for a in (0, 1):
                u_load(a, rel, j, half, slot).wait()
        r = pl.ds(pl.multiple_of(slot * BLK, BLK), BLK)
        phase1(xb, dyb, r, pl.ds(0, BLK))
        transposes(xb, dyb, r, BLK)

        @pl.when(ahead)
        def _():
            other_half(k + 1)
        weight_grads(BLK)

        @pl.when(jnp.logical_and(k >= 2 * PIECES, k < 3 * PIECES - 1))
        def _():
            service(k + 1)
            other_half(k + 1)

        for p in (0, 1):
            @pl.when(k == 2 + 3 * p)
            def _():
                finalize(p, 1)
        return carry
    lax.fori_loop(0, 3 * PIECES, unit, 0)

    grads = (dwg_out, dwu_out, dwd_out)

    def g_part(n, c):
        return acc.at[n, pl.ds(pl.multiple_of(c * ROWS, ROWS), ROWS), :]

    def g_at(n):
        return grads[n].at[:, pl.ds(pl.multiple_of(core * FQ, 128), FQ)]

    g_send = [remote(g_part(n, 1 - core), g_at(n), ds.at[n], dr.at[n], partner) for n in range(3)]
    g_local = [pltpu.make_async_copy(g_part(n, core), g_at(n), dl.at[n]) for n in range(3)]
    for n in range(3):
        g_send[n].start()
        g_local[n].start()

    for m in (0, 1, 2):
        for c in w_direct(m) + w_forward(m):
            c.wait_send()
    for a in (0, 1):
        for j in range(PIECES):
            for k in (0, 1):
                t_own(a, j, k).wait_send()
            t_forward(a, j).wait_send()
            for rel in (1, 2, 3):
                t_share(a, rel, j).wait_send()
    for p in (0, 1):
        for rel in range(4):
            y_zsend(p, rel).wait_send()
        c_send(p).wait_send()
        z_send(p).wait_send()
        for a in (0, 1):
            t_partner(a, p).wait_send()
            b_local(p, a).wait()
            b_send(p, a).wait()
    for n in range(3):
        g_local[n].wait()
        g_send[n].wait()


def write_out(y, dx, g, u, d, y_o, dx_o, g_o, u_o, d_o, yv, dxv, gv, uv, dv, tv, rs, ss):
    loads = [pltpu.make_async_copy(src, dst, rs.at[i])
             for i, (src, dst) in enumerate(((d, dv), (y, yv), (dx, dxv), (g, gv), (u, uv)))]
    stores = [pltpu.make_async_copy(src, dst, ss.at[i])
              for i, (src, dst) in enumerate(((tv, d_o), (yv, y_o), (dxv, dx_o), (gv, g_o), (uv, u_o)))]
    for c in loads:
        c.start()
    loads[0].wait()

    def step(i, carry):
        tv[pl.ds(pl.multiple_of(i * 256, 256), 256), :] = dv[:, pl.ds(pl.multiple_of(i * 256, 256), 256)].T
        return carry
    for i in (1, 2):
        loads[i].wait()
        stores[i].start()
    lax.fori_loop(0, FH // 256, step, 0)
    stores[0].start()
    for i in (3, 4):
        loads[i].wait()
        stores[i].start()
    for c in stores:
        c.wait()


def solution(mesh):
    sds = jax.ShapeDtypeStruct
    dma, vmem = pltpu.SemaphoreType.DMA, pltpu.VMEM

    def device_pass(x, wg, wu, wd, dy):
        anyspec = pl.BlockSpec(memory_space=pl.ANY)
        out = pl.pallas_call(
            kernel,
            out_shape=[sds((TOK, D), BF16), sds((TOK, D), BF16), sds((ROWS, FH), F32), sds((ROWS, FH), F32),
                       sds((ROWS, FH), F32), sds((8, TOK, D), BF16), sds((8, TOK, D), BF16)],
            in_specs=[anyspec] * 5,
            out_specs=[anyspec] * 7,
            scratch_shapes=[
                vmem((D, FQ), BF16), vmem((D, FQ), BF16), vmem((8, FQ, ROWS), BF16),
                vmem((3, 512, FQ), F32),
                vmem((2 * BLK, D), BF16), vmem((2 * BLK, D), BF16),
                vmem((2 * BLK, FQ), BF16), vmem((2 * BLK, FQ), BF16), vmem((2 * BLK, FQ), BF16),
                vmem((2, 2 * BLK, D), F32), vmem((2, 2, BLK, D), F32), vmem((2, 2, 128, D), F32),
                vmem((2 * BLK, D), BF16),
                vmem((512, 2 * BLK), BF16), vmem((512, 2 * BLK), BF16),
                dma((3,)), dma((3, 7)), dma((3, 7)),
                dma((8, 2)), dma((2, 2)), dma((2, 2)),
                dma((PIECES, 2, 2)), dma((PIECES, 2)), dma((4, PIECES, 2)), dma((4, PIECES, 2)), dma((4, PIECES, 2)),
                dma((2, 4)), dma((2, 4)), dma((2, 4)), dma((2, 4)),
                dma((2,)), dma((2,)), dma((2,)), dma((2,)), dma((2, 2)), dma((2, 2)), dma((2, 2)),
                dma((3,)), dma((3,)), dma((3,)),
            ],
            compiler_params=pltpu.CompilerParams(collective_id=0, has_side_effects=True,
                                                 vmem_limit_bytes=67043328),
        )(x, wg, wu, wd, dy)
        shapes = [((TOK, D), BF16)] * 2 + [((ROWS, FH), F32)] * 3
        return pl.pallas_call(
            write_out,
            out_shape=[sds(*s) for s in shapes[:4]] + [sds((FH, ROWS), F32)],
            in_specs=[anyspec] * 5,
            out_specs=[anyspec] * 5,
            scratch_shapes=[vmem(*s) for s in shapes] + [vmem((FH, ROWS), F32), dma((5,)), dma((5,))],
            compiler_params=pltpu.CompilerParams(vmem_limit_bytes=67043328),
        )(*out[:5])

    row_spec = P('dp', None)
    weight_spec = P('dp', 'tp')
    down_spec = P('tp', 'dp')
    return jax.shard_map(device_pass, mesh=mesh,
                         in_specs=(row_spec, weight_spec, weight_spec, down_spec, row_spec),
                         out_specs=(row_spec, row_spec, weight_spec, weight_spec, down_spec),
                         check_vma=False)
```

time: 333 us -> 321 us (0.964)
  local copies, waits for them, and re-layouts: 12.9 us -> 0 us
    unnamed x13 -> x0, local copies, waits for them, and re-layouts: 12.9 us -> none
    pallas_call x0 -> x1, Pallas kernels: none -> 9.45 us  [device_pass(): pl.pallas_call(write_out, out_shape=[sds(*s) for s in shapes[:4]] + [sds(...]
    pallas_call x1, Pallas kernels: 319 us -> 310 us  [device_pass(): pl.pallas_call(kernel, out_shape=[sds((TOK, D), BF16), sds((TOK, D), BF16...]
where the time goes in v2:
time: 321 us
  Pallas kernels  320 us (100%)
    pallas_call x1, Pallas kernels, device_pass(): pl.pallas_call(kernel, out_shape=[sds((TOK, D), BF16), sds((TOK, D), BF16...  310 us
    pallas_call x1, Pallas kernels, device_pass(): pl.pallas_call(write_out, out_shape=[sds(*s) for s in shapes[:4]] + [sds(...  9.45 us

profile of v2, /device:TPU:0, one launch (start us, length us, event | category | flops | bytes accessed | tf_op | source)
XLA Modules:
  0.0 320.6 jit_solution(9417401174588054082)
XLA Ops:
  0.6 310.4 %shard_map.92 = (bf16[512,2048]{1,0:T(8,128)(2,1)}, bf16[512,2048]{1,0:T(8,128)(2,1)}, f32[256,2816]{1,0:T(8,128)}, f32[256,2816]{1,0:T(8,128)}, f32[256,2816]{1...) custom-call(bf16[512,2048]{1,0:T(8,128)(2,1)} %x_in.1, bf16[256,2816]{1,0:T(8,128)(2,1)} %wg_in.1, ...), custom_call_target="tpu_custom_call" | custom-call | tf_op jit(solution)/shard_map/pallas_call | solution.py:509
  311.0 9.4 %shard_map.93 = (bf16[512,2048]{1,0:T(8,128)(2,1)}, bf16[512,2048]{1,0:T(8,128)(2,1)}, f32[256,2816]{1,0:T(8,128)}, f32[256,2816]{1,0:T(8,128)}, f32[2816,256]{1,0:T(8,128)}) custom-call(bf16[512,2048]{1,0:T(8,128)(2,1)} %get-tuple-element.10.y, bf16[512,2048]{1,0:T(8,128)(2,1)} %get-tuple-element.11.dx, f32[256,2816]{1,0:T(8,128)} %get-tuple-element.12.g, ...), custom_call_target="tpu_custom_call" | custom-call | tf_op jit(solution)/shard_map/pallas_call | solution.py:534

commit v3 on v2

--- a/solution.py
+++ b/solution.py
@@ -8,6 +8,7 @@
 from jax.sharding import PartitionSpec as P
 
 MESH = pl.DeviceIdType.MESH
+BOTH = (0, 1)
 BF16, F32 = jnp.bfloat16, jnp.float32
 D, FH, FQ, ROWS, TOK = 2048, 2816, 1408, 256, 512
 SUB, BLK, PIECES = 128, 256, 4
@@ -21,8 +22,8 @@
 
 def kernel(x_in, wg_in, wu_in, wd_in, dy_in,
            y_out, dx_out, dwg_out, dwu_out, dwd_out, x_all, dy_all,
-           wg, wu, wd, acc, xb, dyb, hb, dab, dbb, pb, rc, rz, fb, xt, dyt,
-           wl, ws, wr, xl, os, orr, xs, xf, xd, xr, pr, ys, yr, vs, vr, cs, cr, zs, zr, bs, br, fl, ds, dr, dl):
+           wg, wu, wd, acc, xb, dyb, hb, dab, dbb, pb, rc, rz, fb, xt, dyt, ab,
+           wl, ws, wr, xl, os, orr, es, er, ezs, ezr, xs, xf, xd, xr, pr, ys, yr, vs, vr, cs, cr, zs, zr, bs, br, fl, ds, dr, dl):
     tp, dp = lax.axis_index('tp'), lax.axis_index('dp')
     core, xc, yc = lax.rem(dp, 2), lax.rem(lax.div(dp, 2), 2), lax.div(dp, 4)
     col = lax.div(dp, 2)
@@ -37,7 +38,7 @@
     zdev = (1 - tp, dp)
 
     barrier = pltpu.get_barrier_semaphore()
-    peers = [partner, zdev] + [dev(yc, 1 - xc, cc) for cc in (0, 1)] + [dev(1 - yc, xc, cc) for cc in (0, 1)]
+    peers = [partner, zdev] + [dev(yc, 1 - xc, cc) for cc in BOTH] + [dev(1 - yc, xc, cc) for cc in BOTH]
     for peer in peers:
         pl.semaphore_signal(barrier, inc=1, device_id=peer, device_id_type=MESH)
     pl.semaphore_wait(barrier, len(peers))
@@ -61,7 +62,7 @@
 
     def w_direct(m):
         out = [remote(w_src(m, 1 - core), w_at(m, dp), ws.at[m, 0], wr.at[m, 0], partner)]
-        for cc in (0, 1):
+        for cc in BOTH:
             out.append(remote(w_src(m, cc), w_at(m, dp), ws.at[m, 1 + cc], wr.at[m, 1 + core], dev(yc, 1 - xc, cc)))
             out.append(remote(w_src(m, cc), w_at(m, dp), ws.at[m, 3 + cc], wr.at[m, 3 + core], dev(1 - yc, xc, cc)))
         return out
@@ -114,6 +115,32 @@
                                      bufs[a].at[pl.ds(pl.multiple_of(slot * BLK + half * SUB, SUB), SUB)],
                                      xl.at[4 + slot * 2 + half, a])
 
+    def e_own(a, k):
+        return remote(arrays[a][0].at[rows(0)], t_at(a, 1 + k, core, 0), es.at[k], er.at[1 + k],
+                      (dev(yc, 1 - xc, core), dev(1 - yc, xc, core))[k])
+
+    def e_zshare(a, rel):
+        return remote(t_at(a, rel, core, 0), t_at(a, rel, core, 0), ezs.at[rel], ezr.at[rel], zdev)
+
+    def on_plane(body):
+        for a in BOTH:
+            @pl.when(tp == a)
+            def _(a=a):
+                body(a)
+
+    def e_arrived(rel):
+        def body(a):
+            remote(t_at(a, rel, core, 0), t_at(a, rel, core, 0), ezs.at[rel], er.at[rel], partner).wait_recv()
+            e_zshare(a, rel).start()
+            t_share(a, rel, 0).start()
+        on_plane(body)
+
+    def e_crossed(rel):
+        def body(a):
+            e_zshare(1 - a, rel).wait_recv()
+            t_share(1 - a, rel, 0).start()
+        on_plane(body)
+
     def gates(a, b, g):
         s = jax.nn.sigmoid(a)
         silu = a * s
@@ -121,11 +148,11 @@
 
     main, rest = FQ // 256, pl.ds(FQ // 256 * 256, FQ % 256)
 
-    def tiles(body):
+    def tiles(body, unroll=False):
         def step(n, carry):
             body(pl.ds(pl.multiple_of(n * 256, 256), 256))
             return carry
-        lax.fori_loop(0, main, step, 0)
+        lax.fori_loop(0, main, step, 0, unroll=unroll)
 
     def grad_tile(dy, r, cols):
         g = dot(dy[r, 0:ROWS], wd[0, cols, :], NT)
@@ -137,12 +164,12 @@
         both = dot(x[r, :], jnp.concatenate([wg[:, rest], wu[:, rest]], axis=1), NN)
         return both[:, 0:FQ % 256], both[:, FQ % 256:]
 
-    def phase1(x, dy, r, o):
+    def phase1(x, dy, r, o, unroll=False):
         def body(cols):
             a = dot(x[r, :], wg[:, cols], NN)
             b = dot(x[r, :], wu[:, cols], NN)
             hb[o, cols], dab[o, cols], dbb[o, cols] = gates(a, b, grad_tile(dy, r, cols))
-        tiles(body)
+        tiles(body, unroll)
         a, b = rest_pair(x, r)
         hb[o, rest], dab[o, rest], dbb[o, rest] = gates(a, b, grad_tile(dy, r, rest))
 
@@ -151,7 +178,7 @@
         xt[:, 0:size] = x[r, own_cols].T
         dyt[:, 0:size] = dy[r, own_cols].T
 
-    def weight_grads(size, first=False):
+    def weight_grads(size, first=False, unroll=False):
         o = pl.ds(0, size)
 
         def put(n, cols, value):
@@ -161,7 +188,7 @@
             put(0, cols, dot(xt[:, 0:size], dab[o, cols], NN))
             put(1, cols, dot(xt[:, 0:size], dbb[o, cols], NN))
             put(2, cols, dot(dyt[:, 0:size], hb[o, cols], NN))
-        tiles(body)
+        tiles(body, unroll)
         both = dot(xt[:, 0:size], jnp.concatenate([dab[o, rest], dbb[o, rest]], axis=1), NN)
         put(0, rest, both[:, 0:FQ % 256])
         put(1, rest, both[:, FQ % 256:])
@@ -220,7 +247,7 @@
             cols = pl.ds(pl.multiple_of(i * ROWS, ROWS), ROWS)
             pb[p, :, cols] = dot(dab[...], wg[cols, :], NT) + dot(dbb[...], wu[cols, :], NT)
             return carry
-        lax.fori_loop(0, 8, step, 0)
+        lax.fori_loop(0, 8, step, 0, unroll=2)
         c_send(p).start()
 
     def c_send(p):
@@ -270,15 +297,20 @@
         b_send(p, a).start()
         b_local(p, a).start()
 
+    on_plane(lambda a: [e_own(a, k).start() for k in BOTH])
+    for m in BOTH:
+        for c in w_direct(m):
+            c.start()
     for m in (0, 1, 2):
         w_local(m).start()
-    for m in (0, 1):
-        for c in w_direct(m):
-            c.start()
-    for p in (0, 1):
-        for a in (0, 1):
+    for p in BOTH:
+        for a in BOTH:
             t_partner(a, p).start()
-    for m in (0, 1):
+    e_arrived(1)
+    e_arrived(2)
+    e_crossed(1)
+    e_crossed(2)
+    for m in BOTH:
         w_wait(m, 1)
         w_wait(m, 4)
         for c in w_forward(m):
@@ -286,8 +318,8 @@
     for c in w_direct(2):
         c.start()
 
-    for p in (0, 1):
-        for a in (0, 1):
+    for p in BOTH:
+        for a in BOTH:
             t_partner(a, p).wait_recv()
     first_loads = p_loads(0, 0, xb, 0) + p_loads(1, 0, dyb, 1) + p_loads(0, 1, fb, 2)
     for c in first_loads:
@@ -297,7 +329,7 @@
     everything = pl.ds(0, 2 * BLK)
     transposes(xb, dyb, everything, 2 * BLK)
 
-    for m in (0, 1):
+    for m in BOTH:
         w_local(m).wait()
         for slot in (0, 2, 3, 5, 6):
             w_wait(m, slot)
@@ -321,9 +353,11 @@
     def early1(cols):
         a = dot(fb[...], wg[:, cols], NN)
         b = dot(fb[...], wu[:, cols], NN)
+        ab[0, :, cols], ab[1, :, cols] = a, b
         dbb[:, cols] = silu_up(a, b)
     tiles(early1)
     a, b = rest_pair(fb, everything)
+    ab[0, :, rest], ab[1, :, rest] = a, b
     dbb[:, rest] = silu_up(a, b)
     y_finish(0, 0)
     y_group(1, 0)
@@ -332,10 +366,12 @@
     w_wait(2, 4)
     for c in w_forward(2):
         c.start()
-    for j in range(PIECES):
-        for a in (0, 1):
-            for k in (0, 1):
+    for j in range(1, PIECES):
+        for a in BOTH:
+            for k in BOTH:
                 t_own(a, j, k).start()
+    for a in BOTH:
+        t_forward(a, 0).start()
     y_finish(1, 0)
     w_wait(2, 2)
     y_group(0, 1)
@@ -358,7 +394,7 @@
     tiles(late)
     late(rest)
     y_finish(1, 3)
-    for p in (0, 1):
+    for p in BOTH:
         for rel in range(4):
             y_send(p, rel).wait_send()
     dy1_loads = p_loads(1, 1, xb, 0)
@@ -370,7 +406,12 @@
     for c in dy1_loads:
         c.wait()
     transposes(fb, xb, everything, 2 * BLK)
-    phase1(fb, xb, everything, everything)
+
+    def late1(cols):
+        g = grad_tile(xb, everything, cols)
+        hb[:, cols], dab[:, cols], dbb[:, cols] = gates(ab[0, :, cols], ab[1, :, cols], g)
+    tiles(late1)
+    late1(rest)
     dx_block(1)
     finalize(0, 0)
     weight_grads(2 * BLK)
@@ -378,61 +419,63 @@
     finalize(1, 0)
 
     def unit_of(k):
-        late_unit = k // (2 * PIECES)
-        return ((1 - late_unit) * (1 + lax.rem(k, 2)) + late_unit * 3,
-                (1 - late_unit) * (k // 2) + late_unit * (k - 2 * PIECES))
+        diag = k // (2 * PIECES)
+        return ((1 - diag) * (1 + lax.rem(k, 2)) + diag * 3,
+                (1 - diag) * (k // 2) + diag * (k - 2 * PIECES))
 
     def service(k):
         rel, j = unit_of(k)
         slot = lax.rem(k, 2)
-        for a in (0, 1):
-            t_wait_own(a, rel, j)
-            t_share(a, rel, j).start()
+        for a in BOTH:
+            @pl.when(k > 1)
+            def _(a=a):
+                t_wait_own(a, rel, j)
+                t_share(a, rel, j).start()
             u_load(a, rel, j, 0, slot).start()
 
-        @pl.when(rel == 1 + core)
+        @pl.when(jnp.logical_and(k > 1, rel == 1 + core))
         def _():
-            for a in (0, 1):
+            for a in BOTH:
                 t_forward(a, j).start()
 
     def other_half(k):
         rel, j = unit_of(k)
         slot = lax.rem(k, 2)
-        for a in (0, 1):
+        for a in BOTH:
             t_share(a, rel, j).wait_recv()
             u_load(a, rel, j, 1, slot).start()
 
     service(jnp.int32(0))
     other_half(jnp.int32(0))
+    last = 3 * PIECES - 1
 
     def unit(k, carry):
         rel, j = unit_of(k)
         slot = lax.rem(k, 2)
-        ahead = k < 2 * PIECES
-
-        @pl.when(ahead)
+
+        @pl.when(k < last - 0)
         def _():
             service(k + 1)
 
-        for half in (0, 1):
-            for a in (0, 1):
+        for half in BOTH:
+            for a in BOTH:
                 u_load(a, rel, j, half, slot).wait()
         r = pl.ds(pl.multiple_of(slot * BLK, BLK), BLK)
-        phase1(xb, dyb, r, pl.ds(0, BLK))
+        phase1(xb, dyb, r, pl.ds(0, BLK), True)
         transposes(xb, dyb, r, BLK)
 
-        @pl.when(ahead)
+        @pl.when(k < last - 0)
         def _():
             other_half(k + 1)
-        weight_grads(BLK)
-
-        @pl.when(jnp.logical_and(k >= 2 * PIECES, k < 3 * PIECES - 1))
+        weight_grads(BLK, unroll=True)
+
+        @pl.when(jnp.logical_and(k >= last - 0, k < last))
         def _():
             service(k + 1)
             other_half(k + 1)
 
-        for p in (0, 1):
-            @pl.when(k == 2 + 3 * p)
+        for p in BOTH:
+            @pl.when(k == 4 + 3 * p)
             def _():
                 finalize(p, 1)
         return carry
@@ -455,19 +498,27 @@
     for m in (0, 1, 2):
         for c in w_direct(m) + w_forward(m):
             c.wait_send()
-    for a in (0, 1):
+    for a in BOTH:
         for j in range(PIECES):
-            for k in (0, 1):
-                t_own(a, j, k).wait_send()
+            if j:
+                for k in BOTH:
+                    t_own(a, j, k).wait_send()
             t_forward(a, j).wait_send()
             for rel in (1, 2, 3):
                 t_share(a, rel, j).wait_send()
-    for p in (0, 1):
+
+    def e_drain(a):
+        for k in BOTH:
+            e_own(a, k).wait_send()
+        for rel in (1, 2):
+            e_zshare(a, rel).wait_send()
+    on_plane(e_drain)
+    for p in BOTH:
         for rel in range(4):
             y_zsend(p, rel).wait_send()
         c_send(p).wait_send()
         z_send(p).wait_send()
-        for a in (0, 1):
+        for a in BOTH:
             t_partner(a, p).wait_send()
             b_local(p, a).wait()
             b_send(p, a).wait()
@@ -520,8 +571,10 @@
                 vmem((2, 2 * BLK, D), F32), vmem((2, 2, BLK, D), F32), vmem((2, 2, 128, D), F32),
                 vmem((2 * BLK, D), BF16),
                 vmem((512, 2 * BLK), BF16), vmem((512, 2 * BLK), BF16),
+                vmem((2, 2 * BLK, FQ), F32),
                 dma((3,)), dma((3, 7)), dma((3, 7)),
                 dma((8, 2)), dma((2, 2)), dma((2, 2)),
+                dma((2,)), dma((3,)), dma((3,)), dma((3,)),
                 dma((PIECES, 2, 2)), dma((PIECES, 2)), dma((4, PIECES, 2)), dma((4, PIECES, 2)), dma((4, PIECES, 2)),
                 dma((2, 4)), dma((2, 4)), dma((2, 4)), dma((2, 4)),
                 dma((2,)), dma((2,)), dma((2,)), dma((2,)), dma((2, 2)), dma((2, 2)), dma((2, 2)),

time: 321 us -> 301 us (0.938)
  Pallas kernels: 320 us -> 300 us
    pallas_call x1, Pallas kernels: 310 us -> 291 us  [device_pass(): pl.pallas_call(kernel, out_shape=[sds((TOK, D), BF16), sds((TOK, D), BF16...]
where the time goes in v3:
time: 301 us
  Pallas kernels  300 us (100%)
    pallas_call x1, Pallas kernels, device_pass(): pl.pallas_call(kernel, out_shape=[sds((TOK, D), BF16), sds((TOK, D), BF16...  291 us
    pallas_call x1, Pallas kernels, device_pass(): pl.pallas_call(write_out, out_shape=[sds(*s) for s in shapes[:4]] + [sds(...  9.45 us

profile of v3, /device:TPU:0, one launch (start us, length us, event | category | flops | bytes accessed | tf_op | source)
XLA Modules:
  0.0 301.3 jit_solution(2772562256528579357)
XLA Ops:
  0.6 291.0 %shard_map.92 = (bf16[512,2048]{1,0:T(8,128)(2,1)}, bf16[512,2048]{1,0:T(8,128)(2,1)}, f32[256,2816]{1,0:T(8,128)}, f32[256,2816]{1,0:T(8,128)}, f32[256,2816]{1...) custom-call(bf16[512,2048]{1,0:T(8,128)(2,1)} %x_in.1, bf16[256,2816]{1,0:T(8,128)(2,1)} %wg_in.1, ...), custom_call_target="tpu_custom_call" | custom-call | tf_op jit(solution)/shard_map/pallas_call | solution.py:560
  291.6 9.4 %shard_map.93 = (bf16[512,2048]{1,0:T(8,128)(2,1)}, bf16[512,2048]{1,0:T(8,128)(2,1)}, f32[256,2816]{1,0:T(8,128)}, f32[256,2816]{1,0:T(8,128)}, f32[2816,256]{1,0:T(8,128)}) custom-call(bf16[512,2048]{1,0:T(8,128)(2,1)} %get-tuple-element.10.y, bf16[512,2048]{1,0:T(8,128)(2,1)} %get-tuple-element.11.dx, f32[256,2816]{1,0:T(8,128)} %get-tuple-element.12.g, ...), custom_call_target="tpu_custom_call" | custom-call | tf_op jit(solution)/shard_map/pallas_call | solution.py:587

commit v4 on v3

--- a/solution.py
+++ b/solution.py
@@ -391,7 +391,7 @@
     def late(cols):
         _, dab[:, cols], dbb[:, cols] = gates(pb[0, :, cols], pb[1, :, cols], grad_tile(dyb, everything, cols))
     y_finish(0, 3)
-    tiles(late)
+    tiles(late, True)
     late(rest)
     y_finish(1, 3)
     for p in BOTH:
@@ -410,7 +410,7 @@
     def late1(cols):
         g = grad_tile(xb, everything, cols)
         hb[:, cols], dab[:, cols], dbb[:, cols] = gates(ab[0, :, cols], ab[1, :, cols], g)
-    tiles(late1)
+    tiles(late1, True)
     late1(rest)
     dx_block(1)
     finalize(0, 0)
@@ -453,7 +453,7 @@
         rel, j = unit_of(k)
         slot = lax.rem(k, 2)
 
-        @pl.when(k < last - 0)
+        @pl.when(k < last - 1)
         def _():
             service(k + 1)
 
@@ -464,14 +464,17 @@
         phase1(xb, dyb, r, pl.ds(0, BLK), True)
         transposes(xb, dyb, r, BLK)
 
-        @pl.when(k < last - 0)
+        @pl.when(k < last - 1)
         def _():
             other_half(k + 1)
-        weight_grads(BLK, unroll=True)
-
-        @pl.when(jnp.logical_and(k >= last - 0, k < last))
+
+        @pl.when(k == last - 1)
         def _():
             service(k + 1)
+        weight_grads(BLK, unroll=True)
+
+        @pl.when(k == last - 1)
+        def _():
             other_half(k + 1)
 
         for p in BOTH:

time: 301 us -> 299 us (level)
  no operation moved by 1% of the time
where the time goes in v4:
time: 299 us
  Pallas kernels  298 us (100%)
    pallas_call x1, Pallas kernels, device_pass(): pl.pallas_call(kernel, out_shape=[sds((TOK, D), BF16), sds((TOK, D), BF16...  288 us
    pallas_call x1, Pallas kernels, device_pass(): pl.pallas_call(write_out, out_shape=[sds(*s) for s in shapes[:4]] + [sds(...  9.45 us

profile of v4, /device:TPU:0, one launch (start us, length us, event | category | flops | bytes accessed | tf_op | source)
XLA Modules:
  0.0 298.6 jit_solution(4274461493580199507)
XLA Ops:
  0.6 288.3 %shard_map.92 = (bf16[512,2048]{1,0:T(8,128)(2,1)}, bf16[512,2048]{1,0:T(8,128)(2,1)}, f32[256,2816]{1,0:T(8,128)}, f32[256,2816]{1,0:T(8,128)}, f32[256,2816]{1...) custom-call(bf16[512,2048]{1,0:T(8,128)(2,1)} %x_in.1, bf16[256,2816]{1,0:T(8,128)(2,1)} %wg_in.1, ...), custom_call_target="tpu_custom_call" | custom-call | tf_op jit(solution)/shard_map/pallas_call | solution.py:563
  289.0 9.4 %shard_map.93 = (bf16[512,2048]{1,0:T(8,128)(2,1)}, bf16[512,2048]{1,0:T(8,128)(2,1)}, f32[256,2816]{1,0:T(8,128)}, f32[256,2816]{1,0:T(8,128)}, f32[2816,256]{1,0:T(8,128)}) custom-call(bf16[512,2048]{1,0:T(8,128)(2,1)} %get-tuple-element.10.y, bf16[512,2048]{1,0:T(8,128)(2,1)} %get-tuple-element.11.dx, f32[256,2816]{1,0:T(8,128)} %get-tuple-element.12.g, ...), custom_call_target="tpu_custom_call" | custom-call | tf_op jit(solution)/shard_map/pallas_call | solution.py:590

commit v5 on v4

--- a/solution.py
+++ b/solution.py
@@ -530,26 +530,33 @@
         g_send[n].wait()
 
 
-def write_out(y, dx, g, u, d, y_o, dx_o, g_o, u_o, d_o, yv, dxv, gv, uv, dv, tv, rs, ss):
+def write_out(y, dx, g, u, d, y_o, dx_o, g_o, u_o, d_o, yv, dxv, gv, uv, dv, tv, rs, ss, ts):
     loads = [pltpu.make_async_copy(src, dst, rs.at[i])
              for i, (src, dst) in enumerate(((d, dv), (y, yv), (dx, dxv), (g, gv), (u, uv)))]
     stores = [pltpu.make_async_copy(src, dst, ss.at[i])
-              for i, (src, dst) in enumerate(((tv, d_o), (yv, y_o), (dxv, dx_o), (gv, g_o), (uv, u_o)))]
+              for i, (src, dst) in enumerate(((yv, y_o), (dxv, dx_o), (gv, g_o), (uv, u_o)))]
+    def tile_store(i):
+        part = pl.ds(pl.multiple_of(i * 256, 256), 256)
+        return pltpu.make_async_copy(tv.at[part], d_o.at[part], ts.at[i])
+
+    def step(i, carry):
+        part = pl.ds(pl.multiple_of(i * 256, 256), 256)
+        tv[part, :] = dv[:, part].T
+        tile_store(i).start()
+        return carry
+
+    def done(i, carry):
+        tile_store(i).wait()
+        return carry
+
     for c in loads:
         c.start()
     loads[0].wait()
-
-    def step(i, carry):
-        tv[pl.ds(pl.multiple_of(i * 256, 256), 256), :] = dv[:, pl.ds(pl.multiple_of(i * 256, 256), 256)].T
-        return carry
-    for i in (1, 2):
-        loads[i].wait()
-        stores[i].start()
     lax.fori_loop(0, FH // 256, step, 0)
-    stores[0].start()
-    for i in (3, 4):
-        loads[i].wait()
-        stores[i].start()
+    for load, store in zip(loads[1:], stores):
+        load.wait()
+        store.start()
+    lax.fori_loop(0, FH // 256, done, 0)
     for c in stores:
         c.wait()
 
@@ -592,7 +599,7 @@
             out_shape=[sds(*s) for s in shapes[:4]] + [sds((FH, ROWS), F32)],
             in_specs=[anyspec] * 5,
             out_specs=[anyspec] * 5,
-            scratch_shapes=[vmem(*s) for s in shapes] + [vmem((FH, ROWS), F32), dma((5,)), dma((5,))],
+            scratch_shapes=[vmem(*s) for s in shapes] + [vmem((FH, ROWS), F32), dma((5,)), dma((4,)), dma((FH // 256,))],
             compiler_params=pltpu.CompilerParams(vmem_limit_bytes=67043328),
         )(*out[:5])
 

time: 299 us -> 298 us (level)
  no operation moved by 1% of the time
where the time goes in v5:
time: 298 us
  Pallas kernels  297 us (100%)
    pallas_call x1, Pallas kernels, device_pass(): pl.pallas_call(kernel, out_shape=[sds((TOK, D), BF16), sds((TOK, D), BF16...  288 us
    pallas_call x1, Pallas kernels, device_pass(): pl.pallas_call(write_out, out_shape=[sds(*s) for s in shapes[:4]] + [sds(...  8.98 us

profile of v5, /device:TPU:0, one launch (start us, length us, event | category | flops | bytes accessed | tf_op | source)
XLA Modules:
  0.0 298.1 jit_solution(475433844357641368)
XLA Ops:
  0.6 288.3 %shard_map.92 = (bf16[512,2048]{1,0:T(8,128)(2,1)}, bf16[512,2048]{1,0:T(8,128)(2,1)}, f32[256,2816]{1,0:T(8,128)}, f32[256,2816]{1,0:T(8,128)}, f32[256,2816]{1...) custom-call(bf16[512,2048]{1,0:T(8,128)(2,1)} %x_in.1, bf16[256,2816]{1,0:T(8,128)(2,1)} %wg_in.1, ...), custom_call_target="tpu_custom_call" | custom-call | tf_op jit(solution)/shard_map/pallas_call | solution.py:570
  289.0 9.0 %shard_map.93 = (bf16[512,2048]{1,0:T(8,128)(2,1)}, bf16[512,2048]{1,0:T(8,128)(2,1)}, f32[256,2816]{1,0:T(8,128)}, f32[256,2816]{1,0:T(8,128)}, f32[2816,256]{1,0:T(8,128)}) custom-call(bf16[512,2048]{1,0:T(8,128)(2,1)} %get-tuple-element.10.y, bf16[512,2048]{1,0:T(8,128)(2,1)} %get-tuple-element.11.dx, f32[256,2816]{1,0:T(8,128)} %get-tuple-element.12.g, ...), custom_call_target="tpu_custom_call" | custom-call | tf_op jit(solution)/shard_map/pallas_call | solution.py:597
